TPU v7x, 256 devices: a whole 4x4x8 slice. The times are simulated.
256 devices in a mesh: blk: 4 (over x), grp: 64 (over z, y, core).
Axes of the slice: x: 4, y: 4, z: 8, core: 2. Of those that a mesh axis runs over, the one named last changes fastest.
Arguments:
- points: float32 [3, 32768], P(None, ('blk', 'grp')), may hold values from 0 to 1
- labels: int32 [32768], P(('blk', 'grp')), may hold values 0 or 1
- shape_scale: float32 [32768], P(('blk', 'grp')), may hold values from 0.1 to 0.4
- krylov_basis: float32 [8, 32, 32768], P(None, None, ('blk', 'grp')), may hold values from -6 to 6
- sketch: float32 [1024, 32768], P(None, ('blk', 'grp')), may hold values from -0.03125 to 0.03125
- sketched_basis: float32 [8, 32, 1024], replicated, may hold values from -0.1875 to 0.1875
Outputs:
- next_vector: float32 [32, 32768], P(None, ('blk', 'grp'))
- coefficients: float32 [8, 32], replicated
- sketch_next: float32 [32, 1024], replicated
- norms: float32 [32], replicated
All inputs are finite; a program needn't handle non-finite values. No bound on the sum of `labels` on one device may be relied on, other than what follows from the above.
Results may differ from a plain program's by a relative error of at most 0.0003.
Values sent between devices are 32-bit elements; how exact they have to be, the bound alone decides.
No kernel may reach another device: no remote copies, remote signals or barrier semaphores. Data moves between devices by JAX's collectives and lax.ppermute only.
A program may use at most 64 MiB of HBM per device.

v0:
```python
import functools
import math

import jax
import jax.numpy as jnp
from jax import lax
from jax.experimental import pallas as pl
from jax.experimental.pallas import tpu as pltpu
from jax.sharding import Mesh
from jax.sharding import PartitionSpec as P

SYSTEMS = 32
KRYLOV = 8
FEATS = 32
LANES = 128
X1, X0, Z2, Z1, Z0, Y1, Y0, CORE = ALL = ("x1", "x0", "z2", "z1", "z0", "y1", "y0", "core")
COLUMN = (Z2, Z1, Z0)
ROW = (X1, X0, Y1, Y0)
OWNERS = (X1, X0, Y0, CORE)
LAYERS = (Y1, Y0, Z2, Z1, Z0)
PAIRS = tuple(tuple(8 * y + z for y in pair for z in range(8)) for pair in ((0, 3), (1, 2)))
VMEM = pl.BlockSpec(memory_space=pltpu.VMEM)
MIB = 2**20


def exchange(value, axis):
    return lax.all_to_all(value, axis, 0, 0, tiled=True)


def exchange_layers(value):
    return lax.all_to_all(value, LAYERS, 0, 0, axis_index_groups=PAIRS, tiled=True)


def in_order(value):
    rows = value.shape[0]
    swapped = jnp.concatenate([value[k ^ 4 : (k ^ 4) + 4] for k in range(0, rows, 4)], axis=0)
    return jnp.where(lax.axis_index(Y1) == 1, swapped, value)


def swap(value, axis):
    return lax.ppermute(value, axis, ((0, 1), (1, 0)))


def with_other(value, axis):
    return jnp.concatenate([value, swap(value, axis)], axis=0)


def parts(value):
    first = value.astype(jnp.bfloat16).astype(jnp.float32)
    rest = value - first
    second = rest.astype(jnp.bfloat16).astype(jnp.float32)
    return [first, second, rest - second]


def wide(tiles):
    return jnp.concatenate(tiles, axis=1)


def message_kernel(points_ref, labels_ref, scale_ref, krylov_ref, sources_ref, targets_ref, vector, row, copied, sem):
    taken = [
        pltpu.make_async_copy(krylov_ref.at[krylov_ref.shape[0] - 1], vector, sem.at[0]),
        pltpu.make_async_copy(points_ref, row.at[0:3], sem.at[1]),
        pltpu.make_async_copy(scale_ref, row.at[3:4], sem.at[2]),
        pltpu.make_async_copy(labels_ref, copied, sem.at[3]),
    ]
    for copy in taken:
        copy.start()
    for copy in taken:
        copy.wait()
    for k in range(sources_ref.shape[0]):
        sources_ref[k, 0:SYSTEMS, :] = vector[...]
        sources_ref[k, SYSTEMS : SYSTEMS + 4, :] = row[...]
    targets_ref[0, 0:3, :] = row[0:3, :]
    targets_ref[0, 3:4, :] = copied[...].astype(jnp.float32)


def messages(points, labels, shape_scale, krylov, count):
    hbm = pl.BlockSpec(memory_space=pltpu.HBM)
    return pl.pallas_call(
        message_kernel,
        out_shape=(
            jax.ShapeDtypeStruct((count, SYSTEMS + 4, LANES), jnp.float32),
            jax.ShapeDtypeStruct((1, 4, LANES), jnp.float32),
        ),
        in_specs=[hbm] * 4,
        out_specs=(VMEM,) * 2,
        scratch_shapes=[
            pltpu.VMEM((SYSTEMS, LANES), jnp.float32),
            pltpu.VMEM((4, LANES), jnp.float32),
            pltpu.VMEM((1, LANES), jnp.int32),
            pltpu.SemaphoreType.DMA((4,)),
        ],
        name="messages",
    )(points, labels[None, :], shape_scale[None, :], krylov)


def stored(rows, out_ref):
    zero = jnp.zeros(rows[0].shape, jnp.float32)
    for k, value in enumerate(rows + [zero] * (FEATS - len(rows))):
        out_ref[:, k, :] = value


def pair_of(ref, step):
    return wide([ref[2 * step], ref[2 * step + 1]])


def describe_sources(source_ref, feats_ref, weights_ref):
    coords = [source_ref[:, SYSTEMS + a, :] - 0.5 for a in range(3)]
    scale = source_ref[:, SYSTEMS + 3, :]
    per_square = 1.0 / (scale * scale)
    rows = []
    for value in [c * per_square for c in coords] + [per_square]:
        a, b, c = parts(value)
        rows += [a, a, b, b, a, c]
    square = coords[0] * coords[0] + coords[1] * coords[1] + coords[2] * coords[2]
    stored(rows + parts(square * per_square + 1.0), feats_ref)
    for step in range(weights_ref.shape[0]):
        weight = wide([source_ref[2 * step + j, 0:SYSTEMS, :] for j in range(2)])
        scale = wide([source_ref[2 * step + j, SYSTEMS + 3 : SYSTEMS + 4, :] for j in range(2)])
        terms = []
        for value in (weight / scale, weight * scale):
            first = value.astype(jnp.bfloat16)
            terms += [first, (value - first.astype(jnp.float32)).astype(jnp.bfloat16)]
        weights_ref[step] = jnp.concatenate(terms, axis=0)


def describe_targets(target_ref, feats_ref):
    coords = [target_ref[:, a, :] - 0.5 for a in range(3)]
    square = coords[0] * coords[0] + coords[1] * coords[1] + coords[2] * coords[2]
    rows = []
    for value in [-2.0 * c for c in coords] + [square]:
        a, b, c = parts(value)
        rows += [a, b, a, b, c, a]
    stored(rows + [jnp.ones(square.shape, jnp.float32)] * 3, feats_ref)


def products(sources, target_ref, target_feats):
    indices = range(target_ref.shape[0] // 2)
    feats = [pair_of(target_feats, index).astype(jnp.bfloat16) for index in indices]
    inner = [wide([target_ref[2 * index + j, 3:4, :] for j in range(2)]) > 0.5 for index in indices]
    totals = [jnp.zeros((4 * SYSTEMS, 2 * LANES), jnp.float32) for index in indices]
    for source_feats, weights in sources:
        for step in range(weights.shape[0]):
            source = pair_of(source_feats, step).astype(jnp.bfloat16)
            weight = weights[step]
            for index in indices:
                ratio = lax.dot_general(
                    source, feats[index], (((0,), (0,)), ((), ())), preferred_element_type=jnp.float32
                )
                root = lax.rsqrt(ratio)
                kernel = root * jnp.where(inner[index], 2.0 + root * root, ratio)
                first = kernel.astype(jnp.bfloat16)
                second = (kernel - first.astype(jnp.float32)).astype(jnp.bfloat16)
                totals[index] = (
                    totals[index]
                    + jnp.dot(weight, first, preferred_element_type=jnp.float32)
                    + jnp.dot(weight, second, preferred_element_type=jnp.float32)
                )
    results = []
    for index in indices:
        a, b, c, d = (totals[index][k * SYSTEMS : (k + 1) * SYSTEMS] for k in range(4))
        result = jnp.where(inner[index], a + b, c + d)
        results += [result[:, :LANES], result[:, LANES:]]
    return results


def near_kernel(*refs):
    (source_ref, target_ref, *before, out_ref, source_feats, weights, target_feats) = refs
    describe_sources(source_ref, source_feats, weights)
    describe_targets(target_ref, target_feats)
    for k, part in enumerate(products([(source_feats, weights)], target_ref, target_feats)):
        out_ref[k] = part + before[0][k] if before else part


def far_kernel(first_feats, first_weights, second_feats, second_weights, target_ref, near_ref, out_ref, target_feats):
    describe_targets(target_ref, target_feats)
    place = lax.axis_index(COLUMN)
    near = near_ref.shape[0]
    for k in range(near):
        out_ref[jnp.bitwise_xor(place, k)] = near_ref[k]
    sources = [(first_feats, first_weights), (second_feats, second_weights)]
    for k, part in enumerate(products(sources, target_ref, target_feats)):
        out_ref[jnp.bitwise_xor(place, (near + 2) ^ k)] = part


def cost(sources, targets):
    pairs = sources * targets * LANES * LANES
    return pl.CostEstimate(flops=12 * SYSTEMS * pairs, bytes_accessed=2**20, transcendentals=pairs)


def near_product(sources, targets, *before):
    blocks, owners = sources.shape[0], targets.shape[0]
    return pl.pallas_call(
        near_kernel,
        out_shape=(
            jax.ShapeDtypeStruct((owners, SYSTEMS, LANES), jnp.float32),
            jax.ShapeDtypeStruct((blocks, FEATS, LANES), jnp.float32),
            jax.ShapeDtypeStruct((blocks // 2, 4 * SYSTEMS, 2 * LANES), jnp.bfloat16),
        ),
        in_specs=[VMEM] * (2 + len(before)),
        out_specs=(VMEM,) * 3,
        scratch_shapes=[pltpu.VMEM((owners, FEATS, LANES), jnp.float32)],
        cost_estimate=cost(blocks, owners),
        name="near",
        compiler_params=pltpu.CompilerParams(vmem_limit_bytes=16 * MIB),
    )(sources, targets, *before)


def far_product(described, targets, near):
    blocks, owners = sum(feats.shape[0] for feats in described[::2]), targets.shape[0]
    return pl.pallas_call(
        far_kernel,
        out_shape=jax.ShapeDtypeStruct((owners + near.shape[0], SYSTEMS, LANES), jnp.float32),
        in_specs=[VMEM] * (len(described) + 2),
        out_specs=VMEM,
        scratch_shapes=[pltpu.VMEM((owners, FEATS, LANES), jnp.float32)],
        cost_estimate=cost(blocks, owners),
        name="far",
        compiler_params=pltpu.CompilerParams(vmem_limit_bytes=16 * MIB),
    )(*described, targets, near)


def image_kernel(root, arrived_ref, sketch_ref, image_ref, local_ref):
    total = arrived_ref[0]
    for k in range(1, arrived_ref.shape[0]):
        total = total + arrived_ref[k]
    image = total / root
    image_ref[...] = image
    image = in_order(image)
    first = image.astype(jnp.bfloat16)
    second = (image - first.astype(jnp.float32)).astype(jnp.bfloat16)
    both = jnp.concatenate([first, second], axis=0)
    over_lanes = (((1,), (1,)), ((), ()))
    for k in range(sketch_ref.shape[0] // (2 * LANES)):
        rows = sketch_ref[2 * k * LANES : 2 * (k + 1) * LANES, :]
        high = rows.astype(jnp.bfloat16)
        low = (rows - high.astype(jnp.float32)).astype(jnp.bfloat16)
        total = lax.dot_general(both, high, over_lanes, preferred_element_type=jnp.float32)
        total = total + lax.dot_general(both, low, over_lanes, preferred_element_type=jnp.float32)
        total = total[:SYSTEMS] + total[SYSTEMS:]
        for j in range(2):
            local_ref[:, 2 * k + j, :] = total[:, j * LANES : (j + 1) * LANES]


def image_and_sketch(arrived, sketch, root):
    rows = sketch.shape[0]
    return pl.pallas_call(
        functools.partial(image_kernel, root),
        out_shape=(
            jax.ShapeDtypeStruct((SYSTEMS, LANES), jnp.float32),
            jax.ShapeDtypeStruct((SYSTEMS, rows // LANES, LANES), jnp.float32),
        ),
        in_specs=[VMEM] * 2,
        out_specs=(VMEM,) * 2,
        name="image",
        compiler_params=pltpu.CompilerParams(vmem_limit_bytes=8 * MIB),
    )(arrived, sketch)


def sum_kernel(arrived_ref, out_ref):
    total = arrived_ref[0]
    for k in range(1, arrived_ref.shape[0]):
        total = total + arrived_ref[k]
    for k in range(out_ref.shape[0]):
        out_ref[k] = total


def sum_for_each(arrived, count):
    return pl.pallas_call(
        sum_kernel,
        out_shape=jax.ShapeDtypeStruct((count, *arrived.shape[1:]), jnp.float32),
        in_specs=[VMEM],
        out_specs=VMEM,
        name="addup",
        compiler_params=pltpu.CompilerParams(vmem_limit_bytes=4 * MIB),
    )(arrived)


def project_kernel(share, arrived_ref, basis_ref, out_ref):
    total = arrived_ref[0]
    for k in range(1, arrived_ref.shape[0]):
        total = total + arrived_ref[k]
    rows = total.shape[0] // share
    lane = lax.broadcasted_iota(jnp.int32, (1, LANES), 1)

    def whole(value):
        return jnp.sum(jnp.sum(value, axis=1, keepdims=True), axis=0, keepdims=True)

    lines, last = [], []
    for part in range(share):
        sketched = total[part * rows : (part + 1) * rows]
        basis = [basis_ref[j, part * rows : (part + 1) * rows, :] for j in range(KRYLOV)]
        scalars = jnp.zeros((1, LANES), jnp.float32)
        remainder = sketched
        for j in range(KRYLOV):
            coefficient = whole(basis[j] * sketched)
            scalars = jnp.where(lane == j, coefficient, scalars)
            remainder = remainder - coefficient * basis[j]
        norm = jnp.sqrt(whole(remainder * remainder) / (rows * LANES) + 1e-06)
        lines.append(remainder / norm)
        last.append(jnp.where(lane == KRYLOV, norm, scalars))
    message = jnp.concatenate(lines + last, axis=0)
    for k in range(out_ref.shape[0]):
        for j in range(message.shape[0]):
            out_ref[k, :, j * LANES : (j + 1) * LANES] = message[j : j + 1, :]


def project(arrived, basis, count):
    share = SYSTEMS // count
    return pl.pallas_call(
        functools.partial(project_kernel, share),
        out_shape=jax.ShapeDtypeStruct((count, 1, (arrived.shape[1] + share) * LANES), jnp.float32),
        in_specs=[VMEM] * 2,
        out_specs=VMEM,
        name="project",
        compiler_params=pltpu.CompilerParams(vmem_limit_bytes=4 * MIB),
    )(arrived, basis)


def finish_kernel(arrived_ref, image_ref, krylov_ref, next_ref, coefficients_ref, sketch_ref, norms_ref, lines):
    width, count = sketch_ref.shape[1], arrived_ref.shape[0]
    share = SYSTEMS // count
    for part in range(share):
        place = pl.ds(part, count, stride=share)
        for k in range(width // LANES):
            at = part * width + k * LANES
            lines[k, place, :] = arrived_ref[:, 0, at : at + LANES]
        at = share * width + part * LANES
        lines[width // LANES, place, :] = arrived_ref[:, 0, at : at + LANES]
    for k in range(width // LANES):
        sketch_ref[:, k * LANES : (k + 1) * LANES] = in_order(lines[k])
    scalars = in_order(lines[width // LANES])
    reduced = image_ref[...]
    for j in range(KRYLOV):
        reduced = reduced - scalars[:, j : j + 1] * krylov_ref[j]
    next_ref[...] = reduced / scalars[:, KRYLOV : KRYLOV + 1]
    across = jnp.transpose(scalars)
    coefficients_ref[...] = across[0:KRYLOV, :]
    norms_ref[...] = across[KRYLOV : KRYLOV + 1, :]


def finish(arrived, image, krylov):
    width = arrived.shape[2] * arrived.shape[0] // SYSTEMS - LANES
    return pl.pallas_call(
        finish_kernel,
        out_shape=(
            jax.ShapeDtypeStruct((SYSTEMS, LANES), jnp.float32),
            jax.ShapeDtypeStruct((KRYLOV, SYSTEMS), jnp.float32),
            jax.ShapeDtypeStruct((SYSTEMS, width), jnp.float32),
            jax.ShapeDtypeStruct((1, SYSTEMS), jnp.float32),
        ),
        in_specs=[VMEM] * 3,
        out_specs=(VMEM,) * 4,
        scratch_shapes=[pltpu.VMEM((width // LANES + 1, SYSTEMS, LANES), jnp.float32)],
        name="finish",
        compiler_params=pltpu.CompilerParams(vmem_limit_bytes=8 * MIB),
    )(arrived, image, krylov)


def step(points, labels, shape_scale, krylov_basis, sketch, sketched_basis):
    everything = lax.axis_size(ALL) * points.shape[1]
    system = jnp.bitwise_xor(lax.axis_index(OWNERS), 2 * lax.axis_index(Y1))
    share = SYSTEMS // lax.axis_size(OWNERS)
    basis = lax.dynamic_slice_in_dim(sketched_basis, system * share, share, axis=1)
    basis = basis.reshape(KRYLOV, -1, LANES)
    sources, targets = messages(points, labels, shape_scale, krylov_basis, lax.axis_size(ROW))
    all_sources = exchange(sources, ROW)
    near = with_other(targets, COLUMN[2])
    near = with_other(near, COLUMN[1])
    far = lax.ppermute(near, (Z2, Z1), ((0, 3), (1, 2), (2, 1), (3, 0)))
    near, all_sources, basis = lax.optimization_barrier((near, all_sources, basis))
    other_sources = swap(all_sources, CORE)
    partial_value, *first = near_product(all_sources, near)
    partial_value, *second = near_product(other_sources, near, partial_value)
    partial_value = far_product((*first, *second), far, partial_value)
    image, local_sketch = image_and_sketch(
        exchange(partial_value, COLUMN), sketch, math.sqrt(everything)
    )
    local_sketch = local_sketch.reshape(lax.axis_size(OWNERS), -1, LANES)
    over_owners = sum_for_each(exchange(local_sketch, OWNERS), len(PAIRS[0]))
    message = project(exchange_layers(over_owners), basis, lax.axis_size(OWNERS))
    next_vector, coefficients, sketch_next, norms = finish(
        exchange(message, OWNERS), image, krylov_basis
    )
    return (next_vector, coefficients, sketch_next, norms.reshape(-1))


def solution(mesh):
    torus = Mesh(mesh.devices.reshape((2,) * len(ALL)), ALL)
    in_specs = (P(None, ALL), P(ALL), P(ALL), P(None, None, ALL), P(None, ALL), P())
    out_specs = (P(None, ALL), P(), P(), P())
    return jax.shard_map(step, mesh=torus, in_specs=in_specs, out_specs=out_specs, check_vma=False)
```

profile of v0, /device:TPU:1, one launch (start us, length us, event | category | flops | bytes accessed | tf_op | source)
XLA Modules:
  0.0 78.6 jit_solution(5366536590696056404)
XLA Ops:
  0.6 0.0 copy-start
  0.6 1.6 %messages.1 = (f32[16,36,128]{2,1,0:T(8,128)}, f32[1,4,128]{2,1,0:T(4,128)}) custom-call(f32[3,128]{1,0:T(4,128)} %points_ref.1, s32[1,128]{1,0:T(1,128)} %bitcast.5, f32[1,128]{1,0:T(1,128)} %bitcast.6, f32[8,32,128]{2,1,0:T(8,128)} %krylov_ref.3), custom_call_target="tpu_custom_call" | custom-call | tf_op jit(solution)/shard_map/messages/pallas_call | solution.py:79
  2.2 2.5 %collective-permute-start = (f32[1,4,128]{2,1,0:T(4,128)}, f32[1,4,128]{2,1,0:T(4,128)S(1)}, u32[]{:S(2)}, u32[]{:S(2)}) collective-permute-start(f32[1,4,128]{2,1,0:T(4,128)} %get-tuple-element.21), channel_id=1, source_target_pairs={{0,8},{8,0},{1,9},{9,1},{2,10},{10,2},{3,11},{11,3},{4,12},{12,4},... | collective-permute-start | bytes 6152 | tf_op jit(solution)/shard_map/ppermute | solution.py:41
  4.8 6.8 %all-to-all-start = ((f32[16,36,128]{2,1,0:T(8,128)}), f32[16,36,128]{2,1,0:T(8,128)S(1)}, u32[]{:S(2)}, u32[]{:S(2)}) async-start(f32[16,36,128]{2,1,0:T(8,128)} %get-tuple-element.22), calls=%async_computation | async-start | bytes 655360 | tf_op jit(solution)/shard_map/all_to_all | solution.py:27
  11.6 0.0 copy-done
  11.6 0.0 copy-start.3
  11.6 0.6 copy-done.3
  12.3 0.1 reshape.17.basis_ref
  12.3 0.0 collective-permute-done
  12.3 3.1 %collective-permute-start.1 = (f32[2,4,128]{2,1,0:T(4,128)S(1)}, f32[2,4,128]{2,1,0:T(4,128)S(1)}, u32[]{:S(2)}, u32[]{:S(2)}) collective-permute-start(f32[2,4,128]{2,1,0:T(4,128)S(1)} %pad_maximum_fusion), channel_id=1, source_target_pairs={{0,16},{16,0},{1,17},{17,1},{2,18},{18,2},{3,19},{19,3},{4,20},{20... | collective-permute-start | bytes 12296 | tf_op jit(solution)/shard_map/ppermute | solution.py:41
  15.4 1.0 %collective-permute-done.1 = f32[2,4,128]{2,1,0:T(4,128)S(1)} collective-permute-done((f32[2,4,128]{2,1,0:T(4,128)S(1)}, f32[2,4,128]{2,1,0:T(4,128)S(1)}, u32[]{:S(2)}, u32[]{:S(2)}) %collective-permute-start.1) | collective-permute-done | bytes 4128 | tf_op jit(solution)/shard_map/ppermute | solution.py:41
  16.4 2.9 %all-to-all-done.refs_0_ = f32[16,36,128]{2,1,0:T(8,128)S(1)} async-done(((f32[16,36,128]{2,1,0:T(8,128)}), f32[16,36,128]{2,1,0:T(8,128)S(1)}, u32[]{:S(2)}, u32[]{:S(2)}) %all-to-all-start) | async-done | bytes 294944 | tf_op jit(solution)/shard_map/all_to_all | solution.py:27
  19.4 2.3 %collective-permute-start.2 = (f32[16,36,128]{2,1,0:T(8,128)S(1)}, f32[16,36,128]{2,1,0:T(8,128)S(1)}, u32[]{:S(2)}, u32[]{:S(2)}) collective-permute-start(f32[16,36,128]{2,1,0:T(8,128)S(1)} %all-to-all-done.refs_0_), channel_id=1, source_target_pairs={{0,1},{1,0},{2,3},{3,2},{4,5},{5,4},{6,7},{7,6},{8,9},{9,8},{10,11... | collective-permute-start | bytes 884744 | tf_op jit(solution)/shard_map/ppermute | solution.py:41
  21.7 5.1 %collective-permute-start.3 = (f32[4,4,128]{2,1,0:T(4,128)S(1)}, f32[4,4,128]{2,1,0:T(4,128)S(1)}, u32[]{:S(2)}, u32[]{:S(2)}) collective-permute-start(f32[4,4,128]{2,1,0:T(4,128)S(1)} %constant_dynamic-update-slice_fusion.refs_1_), channel_id=1, source_target_pairs={{0,48},{16,32},{32,16},{48,0},{1,49},{17,33},{33,17},{49,1},{2,50}... | collective-permute-start | bytes 24584 | tf_op jit(solution)/shard_map/ppermute | solution.py:370
  26.8 1.8 %near.2 = (f32[4,32,128]{2,1,0:T(8,128)S(1)}, f32[16,32,128]{2,1,0:T(8,128)S(1)}, bf16[8,128,256]{2,1,0:T(8,128)(2,1)S(1)}) custom-call(f32[16,36,128]{2,1,0:T(8,128)S(1)} %all-to-all-done.refs_0_, f32[4,4,128]{2,1,0:T(4,128)S(1)} %constant_dynamic-update-slice_fusion.refs_1_), custom_call_target="tpu_custom_call" | custom-call | flops 402653184 | bytes 1048576 | tf_op jit(solution)/shard_map/near/pallas_call | solution.py:193
  28.6 0.0 collective-permute-done.2.refs_0_
  28.6 1.8 %near.3 = (f32[4,32,128]{2,1,0:T(8,128)S(1)}, f32[16,32,128]{2,1,0:T(8,128)S(1)}, bf16[8,128,256]{2,1,0:T(8,128)(2,1)S(1)}) custom-call(f32[16,36,128]{2,1,0:T(8,128)S(1)} %collective-permute-done.2.refs_0_, f32[4,4,128]{2,1,0:T(4,128)S(1)} %constant_dynamic-update-slice_fusion.refs_1_, f32[4,32,128]{2,1,0:T(8,128)S(1)} %get-tuple-element.27.refs_2_), custom_call_target="tpu_custom_call" | custom-call | flops 402653184 | bytes 1048576 | tf_op jit(solution)/shard_map/near/pallas_call | solution.py:193
  30.4 0.0 collective-permute-done.3.target_ref
  30.4 0.0 copy-start.1
  30.4 2.7 %far.1 = f32[8,32,128]{2,1,0:T(8,128)S(1)} custom-call(f32[16,32,128]{2,1,0:T(8,128)S(1)} %get-tuple-element.25.first_feats, bf16[8,128,256]{2,1,0:T(8,128)(2,1)S(1)} %get-tuple-element.26.first_weights, f32[16,32,128]{2,1,0:T(8,128)S(1)} %get-tuple-element.28.second_feats, bf16[8,128,256]{2,1,0:T(8,128)(2,1)S(1)} %get-tuple-element.29.second_weights, ...), custom_call_target="tpu_custom_call" | custom-call | flops 805306368 | bytes 1048576 | tf_op jit(solution)/shard_map/far/pallas_call | solution.py:211
  33.2 11.0 %all_to_all.25.arrived_ref = f32[8,32,128]{2,1,0:T(8,128)S(1)} all-to-all(f32[8,32,128]{2,1,0:T(8,128)S(1)} %far.1), channel_id=1, replica_groups=mesh['x1'=2,'x0'=2,'z2'=2,'z1'=2,'z0'=2,'y1'=2,'y0'=2,'core'=2] {'z2','z..., dimensions={0} | all-to-all | bytes 262144 | tf_op jit(solution)/shard_map/all_to_all | solution.py:27
  44.1 0.0 copy-done.1
  44.1 0.3 image.1
  44.5 11.1 %all_to_all.26.arrived_ref = f32[16,16,128]{2,1,0:T(8,128)S(1)} all-to-all(f32[16,16,128]{2,1,0:T(8,128)S(1)} %bitcast.4), channel_id=1, replica_groups=mesh['x1'=2,'x0'=2,'z2'=2,'z1'=2,'z0'=2,'y1'=2,'y0'=2,'core'=2] {'x1','x..., dimensions={0} | all-to-all | bytes 262144 | tf_op jit(solution)/shard_map/all_to_all | solution.py:27
  55.6 11.3 %all_to_all.27.arrived_ref = f32[16,16,128]{2,1,0:T(8,128)S(1)} all-to-all(f32[16,16,128]{2,1,0:T(8,128)S(1)} %addup.1), channel_id=1, replica_groups={{0,8,16,24,32,40,48,56,6,14,22,30,38,46,54,62},{2,10,18,26,34,42,50,58,..., dimensions={0} | all-to-all | bytes 262144 | tf_op jit(solution)/shard_map/all_to_all | solution.py:31
  66.9 0.3 project.1
  67.2 0.0 copy-start.2
  67.2 10.6 %all_to_all.28.arrived_ref = f32[16,1,2304]{2,1,0:T(1,128)S(1)} all-to-all(f32[16,1,2304]{2,1,0:T(1,128)S(1)} %project.1), channel_id=1, replica_groups=mesh['x1'=2,'x0'=2,'z2'=2,'z1'=2,'z0'=2,'y1'=2,'y0'=2,'core'=2] {'x1','x..., dimensions={0} | all-to-all | bytes 294912 | tf_op jit(solution)/shard_map/all_to_all | solution.py:27
  77.8 0.0 copy-done.2
  77.8 0.8 %finish.1 = (f32[32,128]{1,0:T(8,128)}, f32[8,32]{1,0:T(8,128)}, f32[32,1024]{1,0:T(8,128)}, f32[1,32]{1,0:T(1,128)}) custom-call(f32[16,1,2304]{2,1,0:T(1,128)S(1)} %all_to_all.28.arrived_ref, f32[32,128]{1,0:T(8,128)S(1)} %get-tuple-element.33.image_ref, f32[8,32,128]{2,1,0:T(8,128)S(1)} %copy-done.2), custom_call_target="tpu_custom_call" | custom-call | tf_op jit(solution)/shard_map/finish/pallas_call | solution.py:344
  (6 shorter events, 0.1 us)
Async XLA Ops:
  0.6 10.9 %copy-start = (f32[8,32,1024]{2,1,0:T(8,128)S(1)}, f32[8,32,1024]{2,1,0:T(8,128)}, u32[]{:S(2)}) copy-start(f32[8,32,1024]{2,1,0:T(8,128)} %param.11) | copy-start | bytes 3145732
  2.2 10.1 %collective-permute-start = (f32[1,4,128]{2,1,0:T(4,128)}, f32[1,4,128]{2,1,0:T(4,128)S(1)}, u32[]{:S(2)}, u32[]{:S(2)}) collective-permute-start(f32[1,4,128]{2,1,0:T(4,128)} %get-tuple-element.21), channel_id=1, source_target_pairs={{0,8},{8,0},{1,9},{9,1},{2,10},{10,2},{3,11},{11,3},{4,12},{12,4},... | collective-permute-start | bytes 6152 | tf_op jit(solution)/shard_map/ppermute | solution.py:41
  4.8 14.6 %all-to-all-start = ((f32[16,36,128]{2,1,0:T(8,128)}), f32[16,36,128]{2,1,0:T(8,128)S(1)}, u32[]{:S(2)}, u32[]{:S(2)}) async-start(f32[16,36,128]{2,1,0:T(8,128)} %get-tuple-element.22), calls=%async_computation | async-start | bytes 655360 | tf_op jit(solution)/shard_map/all_to_all | solution.py:27
  11.6 0.7 copy-start.3
  12.3 4.1 %collective-permute-start.1 = (f32[2,4,128]{2,1,0:T(4,128)S(1)}, f32[2,4,128]{2,1,0:T(4,128)S(1)}, u32[]{:S(2)}, u32[]{:S(2)}) collective-permute-start(f32[2,4,128]{2,1,0:T(4,128)S(1)} %pad_maximum_fusion), channel_id=1, source_target_pairs={{0,16},{16,0},{1,17},{17,1},{2,18},{18,2},{3,19},{19,3},{4,20},{20... | collective-permute-start | bytes 12296 | tf_op jit(solution)/shard_map/ppermute | solution.py:41
  19.4 9.2 %collective-permute-start.2 = (f32[16,36,128]{2,1,0:T(8,128)S(1)}, f32[16,36,128]{2,1,0:T(8,128)S(1)}, u32[]{:S(2)}, u32[]{:S(2)}) collective-permute-start(f32[16,36,128]{2,1,0:T(8,128)S(1)} %all-to-all-done.refs_0_), channel_id=1, source_target_pairs={{0,1},{1,0},{2,3},{3,2},{4,5},{5,4},{6,7},{7,6},{8,9},{9,8},{10,11... | collective-permute-start | bytes 884744 | tf_op jit(solution)/shard_map/ppermute | solution.py:41
  21.7 8.8 %collective-permute-start.3 = (f32[4,4,128]{2,1,0:T(4,128)S(1)}, f32[4,4,128]{2,1,0:T(4,128)S(1)}, u32[]{:S(2)}, u32[]{:S(2)}) collective-permute-start(f32[4,4,128]{2,1,0:T(4,128)S(1)} %constant_dynamic-update-slice_fusion.refs_1_), channel_id=1, source_target_pairs={{0,48},{16,32},{32,16},{48,0},{1,49},{17,33},{33,17},{49,1},{2,50}... | collective-permute-start | bytes 24584 | tf_op jit(solution)/shard_map/ppermute | solution.py:370
  30.4 13.7 %copy-start.1 = (f32[1024,128]{1,0:T(8,128)S(1)}, f32[1024,128]{1,0:T(8,128)}, u32[]{:S(2)}) copy-start(f32[1024,128]{1,0:T(8,128)} %sketch_ref.1) | copy-start | bytes 1572868
  67.2 10.6 %copy-start.2 = (f32[8,32,128]{2,1,0:T(8,128)S(1)}, f32[8,32,128]{2,1,0:T(8,128)}, u32[]{:S(2)}) copy-start(f32[8,32,128]{2,1,0:T(8,128)} %krylov_ref.3) | copy-start | bytes 393220
where the time goes:
time: 79 us; the launch traced here: 78.6 us
  blocking collectives  43.9 us (56%)
  starting transfers between devices  19.8 us (25%)
  Pallas kernels  9.41 us (12%)
  waiting for transfers between devices  3.92 us (5%)
    all_to_all x3, blocking collectives, exchange(): return lax.all_to_all(value, axis, 0, 0, tiled=True)  32.6 us
    all_to_all x1, blocking collectives, exchange_layers(): lax.all_to_all(value, LAYERS, 0, 0, axis_index_groups=PAIRS, tiled=True)  11.3 us
    ppermute x3, starting transfers between devices, swap(): return lax.ppermute(value, axis, ((0, 1), (1, 0)))  7.94 us
    all_to_all x1, starting transfers between devices, exchange(): return lax.all_to_all(value, axis, 0, 0, tiled=True)  6.75 us
    ppermute x1, starting transfers between devices, step(): far = lax.ppermute(near, (Z2, Z1), ((0, 3), (1, 2), (2, 1), (3, 0)))  5.12 us
    pallas_call x2, Pallas kernels, near_product(): pl.pallas_call(near_kernel, out_shape=(jax.ShapeDtypeStruct((owners, SYST...  3.62 us
    all_to_all x1, waiting for transfers between devices, exchange(): return lax.all_to_all(value, axis, 0, 0, tiled=True)  2.92 us
    pallas_call x1, Pallas kernels, far_product(): pl.pallas_call(far_kernel, out_shape=jax.ShapeDtypeStruct((owners + near....  2.74 us
  transfers between devices with their start and end apart: 5, of which 2 were waited for; matrix products, arithmetic and copies ran while one was open for 0% of the time, Pallas kernels for 5%

commit v1 on v0

--- a/solution.py
+++ b/solution.py
@@ -15,6 +15,7 @@
 LANES = 128
 X1, X0, Z2, Z1, Z0, Y1, Y0, CORE = ALL = ("x1", "x0", "z2", "z1", "z0", "y1", "y0", "core")
 COLUMN = (Z2, Z1, Z0)
+NEAR = (0, 2, 1, 3)
 ROW = (X1, X0, Y1, Y0)
 OWNERS = (X1, X0, Y0, CORE)
 LAYERS = (Y1, Y0, Z2, Z1, Z0)
@@ -177,10 +178,10 @@
     place = lax.axis_index(COLUMN)
     near = near_ref.shape[0]
     for k in range(near):
-        out_ref[jnp.bitwise_xor(place, k)] = near_ref[k]
+        out_ref[jnp.bitwise_xor(place, NEAR[k])] = near_ref[k]
     sources = [(first_feats, first_weights), (second_feats, second_weights)]
     for k, part in enumerate(products(sources, target_ref, target_feats)):
-        out_ref[jnp.bitwise_xor(place, (near + 2) ^ k)] = part
+        out_ref[jnp.bitwise_xor(place, 6 ^ NEAR[k])] = part
 
 
 def cost(sources, targets):
@@ -365,8 +366,8 @@
     basis = basis.reshape(KRYLOV, -1, LANES)
     sources, targets = messages(points, labels, shape_scale, krylov_basis, lax.axis_size(ROW))
     all_sources = exchange(sources, ROW)
-    near = with_other(targets, COLUMN[2])
-    near = with_other(near, COLUMN[1])
+    near = with_other(targets, Z1)
+    near = with_other(near, Z0)
     far = lax.ppermute(near, (Z2, Z1), ((0, 3), (1, 2), (2, 1), (3, 0)))
     near, all_sources, basis = lax.optimization_barrier((near, all_sources, basis))
     other_sources = swap(all_sources, CORE)

time: 79 us -> 79.4 us (level)
  waiting for transfers between devices: 3.92 us -> 5.27 us
  starting transfers between devices: 19.8 us -> 18.9 us
    all_to_all x1, waiting for transfers between devices: 2.92 us -> 4.27 us  [exchange(): return lax.all_to_all(value, axis, 0, 0, tiled=True)]
    ppermute x1, starting transfers between devices: 5.12 us -> 4.2 us  [step(): far = lax.ppermute(near, (Z2, Z1), ((0, 3), (1, 2), (2, 1), (3, 0)))]
where the time goes in v1:
time: 79.4 us; the launch traced here: 79.1 us
  blocking collectives  44 us (55%)
  starting transfers between devices  18.9 us (24%)
  Pallas kernels  9.41 us (12%)
  waiting for transfers between devices  5.27 us (7%)
    all_to_all x3, blocking collectives, exchange(): return lax.all_to_all(value, axis, 0, 0, tiled=True)  32.6 us
    all_to_all x1, blocking collectives, exchange_layers(): lax.all_to_all(value, LAYERS, 0, 0, axis_index_groups=PAIRS, tiled=True)  11.3 us
    ppermute x3, starting transfers between devices, swap(): return lax.ppermute(value, axis, ((0, 1), (1, 0)))  7.94 us
    all_to_all x1, starting transfers between devices, exchange(): return lax.all_to_all(value, axis, 0, 0, tiled=True)  6.75 us
    all_to_all x1, waiting for transfers between devices, exchange(): return lax.all_to_all(value, axis, 0, 0, tiled=True)  4.27 us
    ppermute x1, starting transfers between devices, step(): far = lax.ppermute(near, (Z2, Z1), ((0, 3), (1, 2), (2, 1), (3, 0)))  4.2 us
    pallas_call x2, Pallas kernels, near_product(): pl.pallas_call(near_kernel, out_shape=(jax.ShapeDtypeStruct((owners, SYST...  3.62 us
    pallas_call x1, Pallas kernels, far_product(): pl.pallas_call(far_kernel, out_shape=jax.ShapeDtypeStruct((owners + near....  2.74 us
  transfers between devices with their start and end apart: 5, of which 2 were waited for; matrix products, arithmetic and copies ran while one was open for 0% of the time, Pallas kernels for 5%

profile of v1, /device:TPU:1, one launch (start us, length us, event | category | flops | bytes accessed | tf_op | source)
XLA Modules:
  0.0 79.1 jit_solution(6831731726086628264)
XLA Ops:
  0.6 0.0 copy-start
  0.6 1.6 %messages.1 = (f32[16,36,128]{2,1,0:T(8,128)}, f32[1,4,128]{2,1,0:T(4,128)}) custom-call(f32[3,128]{1,0:T(4,128)} %points_ref.1, s32[1,128]{1,0:T(1,128)} %bitcast.5, f32[1,128]{1,0:T(1,128)} %bitcast.6, f32[8,32,128]{2,1,0:T(8,128)} %krylov_ref.3), custom_call_target="tpu_custom_call" | custom-call | tf_op jit(solution)/shard_map/messages/pallas_call | solution.py:80
  2.2 3.9 %collective-permute-start = (f32[1,4,128]{2,1,0:T(4,128)}, f32[1,4,128]{2,1,0:T(4,128)S(1)}, u32[]{:S(2)}, u32[]{:S(2)}) collective-permute-start(f32[1,4,128]{2,1,0:T(4,128)} %get-tuple-element.21), channel_id=1, source_target_pairs={{0,16},{16,0},{1,17},{17,1},{2,18},{18,2},{3,19},{19,3},{4,20},{20... | collective-permute-start | bytes 6152 | tf_op jit(solution)/shard_map/ppermute | solution.py:42
  6.1 6.8 %all-to-all-start = ((f32[16,36,128]{2,1,0:T(8,128)}), f32[16,36,128]{2,1,0:T(8,128)S(1)}, u32[]{:S(2)}, u32[]{:S(2)}) async-start(f32[16,36,128]{2,1,0:T(8,128)} %get-tuple-element.22), calls=%async_computation | async-start | bytes 655360 | tf_op jit(solution)/shard_map/all_to_all | solution.py:28
  12.9 0.0 copy-done
  12.9 0.0 copy-start.3
  13.0 0.6 copy-done.3
  13.6 0.1 reshape.17.basis_ref
  13.7 0.0 collective-permute-done
  13.7 1.7 %collective-permute-start.1 = (f32[2,4,128]{2,1,0:T(4,128)S(1)}, f32[2,4,128]{2,1,0:T(4,128)S(1)}, u32[]{:S(2)}, u32[]{:S(2)}) collective-permute-start(f32[2,4,128]{2,1,0:T(4,128)S(1)} %pad_maximum_fusion), channel_id=1, source_target_pairs={{0,8},{8,0},{1,9},{9,1},{2,10},{10,2},{3,11},{11,3},{4,12},{12,4},... | collective-permute-start | bytes 12296 | tf_op jit(solution)/shard_map/ppermute | solution.py:42
  15.4 1.0 %collective-permute-done.1 = f32[2,4,128]{2,1,0:T(4,128)S(1)} collective-permute-done((f32[2,4,128]{2,1,0:T(4,128)S(1)}, f32[2,4,128]{2,1,0:T(4,128)S(1)}, u32[]{:S(2)}, u32[]{:S(2)}) %collective-permute-start.1) | collective-permute-done | bytes 4128 | tf_op jit(solution)/shard_map/ppermute | solution.py:42
  16.4 4.3 %all-to-all-done.refs_0_ = f32[16,36,128]{2,1,0:T(8,128)S(1)} async-done(((f32[16,36,128]{2,1,0:T(8,128)}), f32[16,36,128]{2,1,0:T(8,128)S(1)}, u32[]{:S(2)}, u32[]{:S(2)}) %all-to-all-start) | async-done | bytes 294944 | tf_op jit(solution)/shard_map/all_to_all | solution.py:28
  20.7 2.3 %collective-permute-start.2 = (f32[16,36,128]{2,1,0:T(8,128)S(1)}, f32[16,36,128]{2,1,0:T(8,128)S(1)}, u32[]{:S(2)}, u32[]{:S(2)}) collective-permute-start(f32[16,36,128]{2,1,0:T(8,128)S(1)} %all-to-all-done.refs_0_), channel_id=1, source_target_pairs={{0,1},{1,0},{2,3},{3,2},{4,5},{5,4},{6,7},{7,6},{8,9},{9,8},{10,11... | collective-permute-start | bytes 884744 | tf_op jit(solution)/shard_map/ppermute | solution.py:42
  23.0 4.2 %collective-permute-start.3 = (f32[4,4,128]{2,1,0:T(4,128)S(1)}, f32[4,4,128]{2,1,0:T(4,128)S(1)}, u32[]{:S(2)}, u32[]{:S(2)}) collective-permute-start(f32[4,4,128]{2,1,0:T(4,128)S(1)} %constant_dynamic-update-slice_fusion.refs_1_), channel_id=1, source_target_pairs={{0,48},{16,32},{32,16},{48,0},{1,49},{17,33},{33,17},{49,1},{2,50}... | collective-permute-start | bytes 24584 | tf_op jit(solution)/shard_map/ppermute | solution.py:371
  27.2 1.8 %near.2 = (f32[4,32,128]{2,1,0:T(8,128)S(1)}, f32[16,32,128]{2,1,0:T(8,128)S(1)}, bf16[8,128,256]{2,1,0:T(8,128)(2,1)S(1)}) custom-call(f32[16,36,128]{2,1,0:T(8,128)S(1)} %all-to-all-done.refs_0_, f32[4,4,128]{2,1,0:T(4,128)S(1)} %constant_dynamic-update-slice_fusion.refs_1_), custom_call_target="tpu_custom_call" | custom-call | flops 402653184 | bytes 1048576 | tf_op jit(solution)/shard_map/near/pallas_call | solution.py:194
  29.0 0.0 collective-permute-done.2.refs_0_
  29.0 1.8 %near.3 = (f32[4,32,128]{2,1,0:T(8,128)S(1)}, f32[16,32,128]{2,1,0:T(8,128)S(1)}, bf16[8,128,256]{2,1,0:T(8,128)(2,1)S(1)}) custom-call(f32[16,36,128]{2,1,0:T(8,128)S(1)} %collective-permute-done.2.refs_0_, f32[4,4,128]{2,1,0:T(4,128)S(1)} %constant_dynamic-update-slice_fusion.refs_1_, f32[4,32,128]{2,1,0:T(8,128)S(1)} %get-tuple-element.27.refs_2_), custom_call_target="tpu_custom_call" | custom-call | flops 402653184 | bytes 1048576 | tf_op jit(solution)/shard_map/near/pallas_call | solution.py:194
  30.9 0.0 collective-permute-done.3.target_ref
  30.9 0.0 copy-start.1
  30.9 2.7 %far.1 = f32[8,32,128]{2,1,0:T(8,128)S(1)} custom-call(f32[16,32,128]{2,1,0:T(8,128)S(1)} %get-tuple-element.25.first_feats, bf16[8,128,256]{2,1,0:T(8,128)(2,1)S(1)} %get-tuple-element.26.first_weights, f32[16,32,128]{2,1,0:T(8,128)S(1)} %get-tuple-element.28.second_feats, bf16[8,128,256]{2,1,0:T(8,128)(2,1)S(1)} %get-tuple-element.29.second_weights, ...), custom_call_target="tpu_custom_call" | custom-call | flops 805306368 | bytes 1048576 | tf_op jit(solution)/shard_map/far/pallas_call | solution.py:212
  33.6 11.0 %all_to_all.25.arrived_ref = f32[8,32,128]{2,1,0:T(8,128)S(1)} all-to-all(f32[8,32,128]{2,1,0:T(8,128)S(1)} %far.1), channel_id=1, replica_groups=mesh['x1'=2,'x0'=2,'z2'=2,'z1'=2,'z0'=2,'y1'=2,'y0'=2,'core'=2] {'z2','z..., dimensions={0} | all-to-all | bytes 262144 | tf_op jit(solution)/shard_map/all_to_all | solution.py:28
  44.6 0.0 copy-done.1
  44.6 0.3 image.1
  44.9 11.1 %all_to_all.26.arrived_ref = f32[16,16,128]{2,1,0:T(8,128)S(1)} all-to-all(f32[16,16,128]{2,1,0:T(8,128)S(1)} %bitcast.4), channel_id=1, replica_groups=mesh['x1'=2,'x0'=2,'z2'=2,'z1'=2,'z0'=2,'y1'=2,'y0'=2,'core'=2] {'x1','x..., dimensions={0} | all-to-all | bytes 262144 | tf_op jit(solution)/shard_map/all_to_all | solution.py:28
  56.1 11.3 %all_to_all.27.arrived_ref = f32[16,16,128]{2,1,0:T(8,128)S(1)} all-to-all(f32[16,16,128]{2,1,0:T(8,128)S(1)} %addup.1), channel_id=1, replica_groups={{0,8,16,24,32,40,48,56,6,14,22,30,38,46,54,62},{2,10,18,26,34,42,50,58,..., dimensions={0} | all-to-all | bytes 262144 | tf_op jit(solution)/shard_map/all_to_all | solution.py:32
  67.4 0.3 project.1
  67.7 0.0 copy-start.2
  67.7 10.6 %all_to_all.28.arrived_ref = f32[16,1,2304]{2,1,0:T(1,128)S(1)} all-to-all(f32[16,1,2304]{2,1,0:T(1,128)S(1)} %project.1), channel_id=1, replica_groups=mesh['x1'=2,'x0'=2,'z2'=2,'z1'=2,'z0'=2,'y1'=2,'y0'=2,'core'=2] {'x1','x..., dimensions={0} | all-to-all | bytes 294912 | tf_op jit(solution)/shard_map/all_to_all | solution.py:28
  78.3 0.0 copy-done.2
  78.3 0.8 %finish.1 = (f32[32,128]{1,0:T(8,128)}, f32[8,32]{1,0:T(8,128)}, f32[32,1024]{1,0:T(8,128)}, f32[1,32]{1,0:T(1,128)}) custom-call(f32[16,1,2304]{2,1,0:T(1,128)S(1)} %all_to_all.28.arrived_ref, f32[32,128]{1,0:T(8,128)S(1)} %get-tuple-element.33.image_ref, f32[8,32,128]{2,1,0:T(8,128)S(1)} %copy-done.2), custom_call_target="tpu_custom_call" | custom-call | tf_op jit(solution)/shard_map/finish/pallas_call | solution.py:345
  (6 shorter events, 0.1 us)
Async XLA Ops:
  0.6 12.3 %copy-start = (f32[8,32,1024]{2,1,0:T(8,128)S(1)}, f32[8,32,1024]{2,1,0:T(8,128)}, u32[]{:S(2)}) copy-start(f32[8,32,1024]{2,1,0:T(8,128)} %param.11) | copy-start | bytes 3145732
  2.2 11.4 %collective-permute-start = (f32[1,4,128]{2,1,0:T(4,128)}, f32[1,4,128]{2,1,0:T(4,128)S(1)}, u32[]{:S(2)}, u32[]{:S(2)}) collective-permute-start(f32[1,4,128]{2,1,0:T(4,128)} %get-tuple-element.21), channel_id=1, source_target_pairs={{0,16},{16,0},{1,17},{17,1},{2,18},{18,2},{3,19},{19,3},{4,20},{20... | collective-permute-start | bytes 6152 | tf_op jit(solution)/shard_map/ppermute | solution.py:42
  6.1 14.6 %all-to-all-start = ((f32[16,36,128]{2,1,0:T(8,128)}), f32[16,36,128]{2,1,0:T(8,128)S(1)}, u32[]{:S(2)}, u32[]{:S(2)}) async-start(f32[16,36,128]{2,1,0:T(8,128)} %get-tuple-element.22), calls=%async_computation | async-start | bytes 655360 | tf_op jit(solution)/shard_map/all_to_all | solution.py:28
  12.9 0.7 copy-start.3
  13.7 2.7 %collective-permute-start.1 = (f32[2,4,128]{2,1,0:T(4,128)S(1)}, f32[2,4,128]{2,1,0:T(4,128)S(1)}, u32[]{:S(2)}, u32[]{:S(2)}) collective-permute-start(f32[2,4,128]{2,1,0:T(4,128)S(1)} %pad_maximum_fusion), channel_id=1, source_target_pairs={{0,8},{8,0},{1,9},{9,1},{2,10},{10,2},{3,11},{11,3},{4,12},{12,4},... | collective-permute-start | bytes 12296 | tf_op jit(solution)/shard_map/ppermute | solution.py:42
  20.7 8.3 %collective-permute-start.2 = (f32[16,36,128]{2,1,0:T(8,128)S(1)}, f32[16,36,128]{2,1,0:T(8,128)S(1)}, u32[]{:S(2)}, u32[]{:S(2)}) collective-permute-start(f32[16,36,128]{2,1,0:T(8,128)S(1)} %all-to-all-done.refs_0_), channel_id=1, source_target_pairs={{0,1},{1,0},{2,3},{3,2},{4,5},{5,4},{6,7},{7,6},{8,9},{9,8},{10,11... | collective-permute-start | bytes 884744 | tf_op jit(solution)/shard_map/ppermute | solution.py:42
  23.0 7.8 %collective-permute-start.3 = (f32[4,4,128]{2,1,0:T(4,128)S(1)}, f32[4,4,128]{2,1,0:T(4,128)S(1)}, u32[]{:S(2)}, u32[]{:S(2)}) collective-permute-start(f32[4,4,128]{2,1,0:T(4,128)S(1)} %constant_dynamic-update-slice_fusion.refs_1_), channel_id=1, source_target_pairs={{0,48},{16,32},{32,16},{48,0},{1,49},{17,33},{33,17},{49,1},{2,50}... | collective-permute-start | bytes 24584 | tf_op jit(solution)/shard_map/ppermute | solution.py:371
  30.9 13.7 %copy-start.1 = (f32[1024,128]{1,0:T(8,128)S(1)}, f32[1024,128]{1,0:T(8,128)}, u32[]{:S(2)}) copy-start(f32[1024,128]{1,0:T(8,128)} %sketch_ref.1) | copy-start | bytes 1572868
  67.7 10.6 %copy-start.2 = (f32[8,32,128]{2,1,0:T(8,128)S(1)}, f32[8,32,128]{2,1,0:T(8,128)}, u32[]{:S(2)}) copy-start(f32[8,32,128]{2,1,0:T(8,128)} %krylov_ref.3) | copy-start | bytes 393220
